TPU v7x, 32 devices: a whole 2x2x4 slice. The times are simulated.
32 devices in a mesh: dp: 8 (over z, y), tensor: 4 (over x, core).
Axes of the slice: x: 2, y: 2, z: 4, core: 2. Of those that a mesh axis runs over, the one named last changes fastest.
Arguments:
- hidden: bfloat16 [8, 1024, 1024], P('dp', 'tensor'), may hold values from -6 to 6
- encoder: bfloat16 [8, 1024, 1024], P('dp', 'tensor'), may hold values from -6 to 6
- prefix: int32 [8], P('dp'), may hold values from 102 to 512
- query_self: bfloat16 [1, 1024, 1024], P(None, 'dp', 'tensor'), may hold values from -0.1875 to 0.1875
- key_self: bfloat16 [1, 1024, 1024], P(None, 'dp', 'tensor'), may hold values from -0.1875 to 0.1875
- value_self: bfloat16 [1, 1024, 1024], P(None, 'dp', 'tensor'), may hold values from -0.1875 to 0.1875
- output_self: bfloat16 [1, 1024, 1024], P(None, 'tensor', 'dp'), may hold values from -3 to 3
- cross_query_matrix: bfloat16 [1, 1024, 1024], P(None, 'dp', 'tensor'), may hold values from -0.1875 to 0.1875
- key_cross: bfloat16 [1, 1024, 1024], P(None, 'dp', 'tensor'), may hold values from -0.1875 to 0.1875
- value_cross: bfloat16 [1, 1024, 1024], P(None, 'dp', 'tensor'), may hold values from -0.1875 to 0.1875
- output_cross: bfloat16 [1, 1024, 1024], P(None, 'tensor', 'dp'), may hold values from -3 to 3
- expand: bfloat16 [1, 1024, 4096], P(None, 'dp', 'tensor'), may hold values from -0.1875 to 0.1875
- shrink: bfloat16 [1, 4096, 1024], P(None, 'tensor', 'dp'), may hold values from -0.09375 to 0.09375
- norm_gains: float32 [1, 3, 1024], replicated, may hold values from 0.25 to 1.75
- biases: float32 [1, 9, 1024], replicated, may hold values from -1.8 to 1.8
- self_out_bias: float32 [1, 1024], replicated, may hold values from -1.8 to 1.8
- expand_bias: float32 [1, 4096], replicated, may hold values from -1.8 to 1.8
- cotangent: bfloat16 [8, 1024, 1024], P('dp', 'tensor'), may hold values from -6 to 6
Outputs:
- block_output: bfloat16 [8, 1024, 1024], P('dp', 'tensor')
- grad_hidden: float32 [8, 1024, 1024], P('dp', 'tensor')
- grad_encoder: float32 [8, 1024, 1024], P('dp', 'tensor')
- grad_query_self: float32 [1, 1024, 1024], P(None, 'dp', 'tensor')
- grad_key_self: float32 [1, 1024, 1024], P(None, 'dp', 'tensor')
- grad_value_self: float32 [1, 1024, 1024], P(None, 'dp', 'tensor')
- grad_output_self: float32 [1, 1024, 1024], P(None, 'tensor', 'dp')
- grad_query_cross: float32 [1, 1024, 1024], P(None, 'dp', 'tensor')
- grad_key_cross: float32 [1, 1024, 1024], P(None, 'dp', 'tensor')
- grad_value_cross: float32 [1, 1024, 1024], P(None, 'dp', 'tensor')
- grad_output_cross: float32 [1, 1024, 1024], P(None, 'tensor', 'dp')
- grad_expand: float32 [1, 1024, 4096], P(None, 'dp', 'tensor')
- grad_shrink: float32 [1, 4096, 1024], P(None, 'tensor', 'dp')
- grad_norm_gains: float32 [1, 3, 1024], replicated
- grad_biases: float32 [1, 9, 1024], replicated
- grad_self_out_bias: float32 [1, 1024], replicated
- grad_expand_bias: float32 [1, 4096], replicated
Inputs may be any that keep to these rules, and one draw needn't show every extreme that they name: prefix[b] leading tokens of sequence b are seen by every token of it.
All inputs are finite; a program needn't handle non-finite values.
Results may differ from a plain program's by a relative error of at most 0.024.
Values may be sent and summed in bfloat16 or wider, within the bound.
A program may use at most 192 MiB of HBM per device.

v0:
```python
import functools

import jax
import jax.numpy as jnp
from jax import lax
from jax.experimental import pallas as pl
from jax.experimental.pallas import tpu as pltpu
from jax.sharding import PartitionSpec as P

MESH = pl.DeviceIdType.MESH
BF = jnp.bfloat16
F32 = jnp.float32
EPS = 1e-05
HEAD = 64
LOG2E = 1.4426950408889634
LN2 = 0.6931471805599453
NEG = -1e30
SMALL_ROWS = 24


def dot(a, b, ca, cb):
    return lax.dot_general(a, b, (((ca,), (cb,)), ((), ())), preferred_element_type=F32)


def layer_kernel(nz, sh, *refs):
    (
        prefix,
        hid,
        enc,
        cot,
        q_in,
        k_in,
        v_in,
        o_in,
        k2_in,
        v2_in,
        q2_in,
        o2_in,
        we_in,
        ws_in,
        gains,
        biases,
        selfb,
        expb,
        block_out,
        hid_out,
        enc_out,
        ge_out,
        gs_out,
        gc_out,
        ga_out,
        gain_out,
        bias_out,
        selfb_out,
        expb_out,
        xland,
        eland,
        cland,
        yland,
        zland,
        wa,
        wb,
        wc,
        we,
        ws,
        x1r,
        x2r,
        ct,
        qs,
        ks,
        vs,
        ao,
        q2,
        k2,
        v2,
        a2,
        gg,
        gp,
        n1,
        n2,
        r1,
        r2,
        lse1,
        lse2,
        res,
        sx,
        rx,
        rxd,
        dq,
        do,
        dk,
        dv,
        ksend,
        krecv,
        cs,
        own,
        tmp,
        xt,
        dom,
        qm,
        den,
        outf,
        sm,
        smr,
        smz,
        sems,
    ) = refs
    d = lax.axis_index("dp")
    t = lax.axis_index("tensor")
    x, c = t // 2, t % 2
    z, y = d // 2, d % 2
    nx, nc, ny = 1 - x, 1 - c, 1 - y
    x_dev = (d, nx * 2 + c)
    c_dev = (d, x * 2 + nc)
    y_dev = (z * 2 + ny, t)

    def z_dev(k):
        return (lax.rem(z + k, nz) * 2 + y, t)

    def z_from(k):
        return lax.rem(z + nz - k, nz)

    nq = nz // 4
    rows = hid.shape[0]
    count = [0]

    def new_sem():
        count[0] += 1
        return sems.at[count[0] - 1]

    pending = []

    def plan(src, dst, dev):
        return pltpu.make_async_remote_copy(
            src_ref=src, dst_ref=dst, send_sem=new_sem(), recv_sem=new_sem(), device_id=dev, device_id_type=MESH
        )

    def launch(cp):
        cp.start()
        pending.append(cp)
        return cp

    def send(src, dst, dev):
        return launch(plan(src, dst, dev))

    def sent(cp):
        cp.wait_send()
        pending[:] = [other for other in pending if other is not cp]

    def local(src, dst):
        cp = pltpu.make_async_copy(src, dst, new_sem())
        cp.start()
        return cp

    barrier = pltpu.get_barrier_semaphore()
    peers = [x_dev, c_dev, y_dev] + [z_dev(k) for k in range(1, nz)]
    for dev in peers:
        pl.semaphore_signal(barrier, inc=1, device_id=dev, device_id_type=MESH)
    pl.semaphore_wait(barrier, len(peers))

    xs = [send(hid, xland.at[x], x_dev)]
    groups = {
        "a": ([q_in, k_in, v_in], wa),
        "b": ([o_in, k2_in, v2_in], wb),
        "c": ([q2_in, o2_in], wc),
        "e": ([we_in], we),
        "s": ([ws_in], ws),
    }

    class Bundle:
        def __init__(self, copies):
            self.copies = copies

        def start(self):
            for cp in self.copies:
                cp.start()

        def wait_recv(self):
            for cp in self.copies:
                cp.wait_recv()

        def wait_send(self):
            for cp in self.copies:
                cp.wait_send()

        def wait(self):
            for cp in self.copies:
                cp.wait()

    def columns_of(srcs, g, spot):
        width = srcs[0].shape[1]
        buf = groups[g][1]
        for i, src in enumerate(srcs):
            yield src, buf.at[(*spot, slice(None), slice(i * width, i * width + width))]

    def plan_own(g, dev):
        return Bundle([plan(src, dst, dev) for src, dst in columns_of(groups[g][0], g, (c, z, y))])

    zc, yc, cz, cy, lc = {}, {}, {}, {}, {}
    peers_z = range(1, nz)

    for g in groups:
        buf = groups[g][1]
        zc[g] = {k: plan_own(g, z_dev(k)) for k in peers_z}
        yc[g] = {0: plan_own(g, y_dev)}
        cz[g] = {0: plan_own(g, c_dev)}
        cy[g] = {}
        for k in range(nz):
            zk = z_from(k)
            if k:
                spot = buf.at[c, zk, y]
                yc[g][k] = plan(spot, spot, y_dev)
                cz[g][k] = plan(spot, spot, c_dev)
            spot = buf.at[c, zk, ny]
            cy[g][k] = plan(spot, spot, c_dev)

    def start_z(g):
        for k in peers_z:
            launch(zc[g][k])

    def start_y(g):
        launch(yc[g][0])

    def start_c(g):
        launch(cz[g][0])
        lc[g] = Bundle([local(src, dst) for src, dst in columns_of(groups[g][0], g, (c, z, y))])

    def thirds(part):
        return range(1 + (nz - 1) * part // 3, 1 + (nz - 1) * (part + 1) // 3)

    def z_event(g, part):
        for k in thirds(part):
            zc[g][k].wait_recv()
            launch(yc[g][k])
            launch(cz[g][k])

    def y_event(g, part):
        for k in [0] if part < 0 else thirds(part):
            yc[g][k].wait_recv()
            launch(cy[g][k])

    def c_event(g):
        lc[g].wait()
        for cp in list(cz[g].values()) + list(cy[g].values()):
            cp.wait_recv()

    def run(*words):
        for word in words:
            kind, g, part = word[0], word[1], int(word[2:] or 0)
            if kind == "o":
                start_y(g)
            else:
                (z_event if kind == "z" else y_event)(g, part)

    start_z("a")
    start_y("a")
    start_c("a")
    l_x = local(hid, x1r.at[x])
    l_e = local(enc, x2r.at[x])
    l_c = local(cot, ct.at[x])
    start_z("b")
    start_y("b")
    start_c("b")
    xs.append(send(enc, eland.at[x], x_dev))
    xs.append(send(cot, ct.at[x], x_dev))
    for g in ("c", "e", "s"):
        start_z(g)
        start_c(g)

    def hooked(hooks, i):
        for at, text in hooks.items():
            if isinstance(text, tuple):
                pl.when(i == at // 2 * 2)(functools.partial(run, *text))
            else:
                pl.when(i == at // 2 * 2)(text)

    def w_all(buf, q, lo, hi):
        return buf[q, :, :, :, lo:hi].reshape(1024, hi - lo)

    def bias_at(ref, row, lo, width):
        return ref[row, :, pl.ds(pl.multiple_of(lo, 256), width)]

    sm[...] = jnp.zeros_like(sm)

    def fold(v):
        return jnp.sum(v.reshape(v.shape[0] // 8, 8, v.shape[1]), axis=0)

    scale = HEAD**-0.5

    l_x.wait()
    xs[0].wait_recv()
    l_xn = local(xland.at[nx], x1r.at[nx])
    run("za0", "ya-1", "za1", "ya0", "za2", "oc", "ya1", "ya2")
    l_xn.wait()
    c_event("a")
    kv1 = []
    for j in range(2):
        xj = x1r[j]
        for q in range(2):
            r = dot(xj, w_all(wa, q, 0, 768), 1, 0)
            lanes = slice(q * 256, q * 256 + 256)
            col = x * 512 + q * 256
            qs[j, :, lanes] = ((r[:, :256] + bias_at(biases, 0, col, 256)) * (scale * LOG2E)).astype(BF)
            ks[2 * j + c, :, lanes] = r[:, 256:512].astype(BF)
            vs[2 * j + c, :, lanes] = (r[:, 512:] + bias_at(biases, 1, col, 256)).astype(BF)
        kv1 += [send(b.at[2 * j + c], b.at[2 * j + c], c_dev) for b in (ks, vs)]
        run(*(("zb0", "oe") if j == 0 else ("zb1",)))
    xs[1].wait_recv()
    l_en = local(eland.at[nx], x2r.at[nx])

    lane256 = lax.broadcasted_iota(jnp.int32, (128, 256), 1)
    lane128 = lax.broadcasted_iota(jnp.int32, (128, 128), 1)
    zero_bf = jnp.zeros((128, 256), BF)
    lane256w = lax.broadcasted_iota(jnp.int32, (256, 256), 1)
    lane128w = lax.broadcasted_iota(jnp.int32, (256, 128), 1)
    zero_bfw = jnp.zeros((256, 256), BF)
    limit = prefix[0]

    def parts_of(keys, causal, j):
        if not causal:
            return [(0, 4, False)]
        return [(0, 2, True)] if j == 0 else [(0, 2, False), (2, 4, True)]

    def scores(qh, k_ref, part, lanes, j, row0):
        b0, b1, masked = part
        k = k_ref[b0:b1, :, lanes].reshape((b1 - b0) * 256, 256)
        s = dot(qh, k, 1, 1)
        if masked:
            cols = b0 * 256 + lax.broadcasted_iota(jnp.int32, s.shape, 1)
            rws = (2 * j + c) * 256 + row0 + lax.broadcasted_iota(jnp.int32, s.shape, 0)
            s = jnp.where((cols <= rws) | (cols < limit), s, NEG)
        return s

    def attend(j, q_ref, k_ref, v_ref, o_ref, l_ref, causal, hooks):
        parts = parts_of(k_ref, causal, j)

        def body(i, carry):
            hooked(hooks, 2 * i)
            h = i
            row0 = 0
            rws = slice(0, 256)
            lanes = pl.ds(pl.multiple_of((h // 4) * 256, 256), 256)
            head = (lane256w // HEAD) == (h % 4)
            qh = jnp.where(head, q_ref[j, rws, lanes], zero_bfw)
            ss = [scores(qh, k_ref, p, lanes, j, row0) for p in parts]
            m = functools.reduce(jnp.maximum, [jnp.max(s, axis=1, keepdims=True) for s in ss])
            total = jnp.zeros((256, 1), F32)
            o = jnp.zeros((256, 256), F32)
            for s, (b0, b1, _) in zip(ss, parts):
                p = jnp.exp2(s - m)
                total = total + jnp.sum(p, axis=1, keepdims=True)
                o = o + dot(p.astype(BF), v_ref[b0:b1, :, lanes].reshape((b1 - b0) * 256, 256), 1, 0)
            o = o / total
            o_ref[j, rws, lanes] = jnp.where(head, o.astype(BF), o_ref[j, rws, lanes])
            l_ref[j, rws, :] = jnp.where(lane128w == h, m + jnp.log2(total), l_ref[j, rws, :])
            return carry

        lax.fori_loop(0, 8, body, 0)

    def attend_back(j, q_ref, k_ref, v_ref, o_ref, l_ref, causal, hooks):
        parts = parts_of(k_ref, causal, j)
        nk = 256 * parts[-1][1]
        for qt in range(2):
            lanes = slice(qt * 256, qt * 256 + 256)

            def body(i, carry):
                hooked(hooks[qt], 2 * i)
                h = i
                row0 = 0
                rws = slice(0, 256)
                spot = pl.ds(pl.multiple_of(i * 256, 256), 256)
                head = (lane256w // HEAD) == h
                qh = jnp.where(head, q_ref[j, rws, lanes], zero_bfw)
                dh = jnp.where(head, do[rws, lanes], zero_bfw)
                delta = jnp.sum(dh.astype(F32) * o_ref[j, rws, lanes].astype(F32), axis=1, keepdims=True)
                lse = jnp.sum(jnp.where(lane128w == h + 4 * qt, l_ref[j, rws, :], 0.0), axis=1, keepdims=True)
                g = jnp.zeros((256, 256), F32)
                for part in parts:
                    b0, b1, _ = part
                    s = scores(qh, k_ref, part, lanes, j, row0)
                    p = jnp.exp2(s - lse)
                    dp = dot(dh, v_ref[b0:b1, :, lanes].reshape((b1 - b0) * 256, 256), 1, 1)
                    ds = (p * (dp - delta)).astype(BF)
                    cs[0, spot, b0 * 256 : b1 * 256] = p.astype(BF)
                    cs[1, spot, b0 * 256 : b1 * 256] = ds
                    g = g + dot(ds, k_ref[b0:b1, :, lanes].reshape((b1 - b0) * 256, 256), 1, 0)
                dq[j, rws, lanes] = jnp.where(head, (g.astype(BF) * scale).astype(BF), dq[j, rws, lanes])
                dom[spot, :] = dh
                qm[spot, :] = qh
                return carry

            lax.fori_loop(0, 4, body, 0)
            for b in range(nk // 256):
                keys = slice(b * 256, b * 256 + 256)
                gv = dot(cs[0, :, keys], dom[...], 0, 0)
                gk = dot(cs[1, :, keys], qm[...], 0, 0) * LN2
                if j == 0:
                    dv[b, :, lanes] = gv
                    dk[b, :, lanes] = gk
                else:
                    dv[b, :, lanes] += gv
                    dk[b, :, lanes] += gk
        if j == 0 and nk < 1024:
            dv[2:4] = jnp.zeros((2, 256, 512), F32)
            dk[2:4] = jnp.zeros((2, 256, 512), F32)

    def over_columns(body):
        def step(dn, carry):
            body(dn, pl.ds(pl.multiple_of(dn * 256, 256), 256))
            return carry

        lax.fori_loop(0, 4, step, 0)

    def rows_at(buf, q, dn, lo, hi):
        return buf[q, pl.ds(dn * nq, nq), :, :, lo:hi].reshape(256, hi - lo)

    def project_out(j, src, buf, lo):
        def body(dn, cols):
            acc = dot(src[j, :, 0:256], rows_at(buf, 0, dn, lo, lo + 256), 1, 1)
            acc = acc + dot(src[j, :, 256:512], rows_at(buf, 1, dn, lo, lo + 256), 1, 1)
            sx[j, :, cols] = acc.astype(BF)

        over_columns(body)

    ex = {}

    def exchange(stage, j):
        ex[stage, j] = send(sx.at[j], rx.at[stage % 2, j], x_dev)

    def arrived(stage, j):
        ex[stage, j].wait_recv()
        sent(ex[stage, j])

    TILE = 32

    def norm_forward(j, stage, base, bias, gain, shift, n_ref, r_ref, low_ref):
        def body(i, carry):
            rws = pl.ds(pl.multiple_of(i * TILE, TILE), TILE)
            v = base[j, rws, :].astype(F32) + sx[j, rws, :].astype(F32) + rx[stage % 2, j, rws, :].astype(F32) + bias
            cen = v - jnp.mean(v, axis=1, keepdims=True)
            r = lax.rsqrt(jnp.mean(cen * cen, axis=1, keepdims=True) + EPS)
            n = cen * r
            o = n * gain + shift
            n_ref[j, rws, :] = n.astype(BF)
            r_ref[j, rws, :] = jnp.broadcast_to(r, (TILE, 128))
            res[j, rws, :] = o
            low_ref[j, rws, :] = o.astype(BF)
            return carry

        lax.fori_loop(0, rows // TILE, body, 0)

    def add_small(row, v):
        sm[row : row + 1, :] += jnp.sum(v, axis=0, keepdims=True) * 0.5

    def back_tile(dz, n, r, gain):
        gz = gain * dz
        ma = jnp.mean(gz, axis=1, keepdims=True)
        mb = jnp.mean(gz * n, axis=1, keepdims=True)
        return (gz - ma - n * mb) * r

    def norm_back(j, stage, gain, n_ref, r_ref, gain_row, shift_row, bias_row):
        def body(i, carry):
            sa, sb, sc = carry
            rws = pl.ds(pl.multiple_of(i * TILE, TILE), TILE)
            dz = res[j, rws, :] + sx[j, rws, :].astype(F32) + rx[stage % 2, j, rws, :].astype(F32)
            n = n_ref[j, rws, :].astype(F32)
            dt = back_tile(dz, n, r_ref[j, rws, 0:1], gain)
            res[j, rws, :] = dt
            ct[j, rws, :] = dt.astype(BF)
            return sa + fold(dz * n), sb + fold(dz), sc + fold(dt)

        zero = jnp.zeros((8, 1024), F32)
        sa, sb, sc = lax.fori_loop(0, rows // TILE, body, (zero, zero, zero))
        add_small(gain_row, sa)
        add_small(shift_row, sb)
        add_small(bias_row, sc)

    for cp in kv1:
        cp.wait_recv()
    attend(0, qs, ks, vs, ao, lse1, True, {5: ("zb2",), 14: ("zc0", "os",)})
    run("yb-1", "yb0", "yb1", "zc1", "yb2")
    c_event("b")
    project_out(0, ao, wb, 0)
    exchange(0, 0)
    attend(1, qs, ks, vs, ao, lse1, True, {4: ("zc2",), 13: ("yc-1", "yc0",)})
    project_out(1, ao, wb, 0)
    exchange(0, 1)
    run("ze0", "yc1", "yc2")
    l_e.wait()
    l_en.wait()
    def encoder_part(i, carry):
        j, q = i // 2, i % 2
        r = dot(x2r[j], w_all(wb, q, 256, 768), 1, 0)
        lanes = pl.ds(pl.multiple_of(q * 256, 256), 256)
        k2[2 * j + c, :, lanes] = r[:, :256].astype(BF)
        v2[2 * j + c, :, lanes] = (r[:, 256:] + bias_at(biases, 3, x * 512 + q * 256, 256)).astype(BF)
        return carry

    lax.fori_loop(0, 4, encoder_part, 0)
    kv2 = [send(b.at[2 * j + c], b.at[2 * j + c], c_dev) for j in range(2) for b in (k2, v2)]
    c_event("c")
    for cp in kv2:
        cp.wait_recv()

    def cross(j, hooks):
        arrived(0, j)
        norm_forward(j, 0, x1r, selfb[0:1, :], gains[0], biases[6], n1, r1, x1r)

        def body(q, carry):
            r = dot(x1r[j], w_all(wc, q, 0, 256), 1, 0) + bias_at(biases, 2, x * 512 + q * 256, 256)
            q2[j, :, pl.ds(pl.multiple_of(q * 256, 256), 256)] = (r * (scale * LOG2E)).astype(BF)
            return carry

        lax.fori_loop(0, 2, body, 0)
        attend(j, q2, k2, v2, a2, lse2, False, hooks)
        project_out(j, a2, wc, 256)
        exchange(1, j)

    cross(0, {1: ("ze1",), 12: ("ze2",)})
    cross(1, {1: ("zs0",), 6: ("ye-1", "ye0", "ye1",), 12: ("zs1",)})

    root_half = 0.7071067811865476
    norm_pdf = 0.3989422804014327

    def hidden_units(j):
        arrived(1, j)
        norm_forward(j, 1, res, biases[4], gains[1], biases[7], n2, r2, x2r)

        def body(step, carry):
            q, i = step // 4, step % 4
            lanes = pl.ds(pl.multiple_of(i * 256, 256), 256)
            h = dot(x2r[j], we[q, :, :, :, lanes].reshape(1024, 256), 1, 0)
            h = h + expb[0:1, pl.ds(pl.multiple_of(x * 2048 + step * 256, 256), 256)]
            cdf = 0.5 * (1.0 + lax.erf(h * root_half))
            gg[q, j, :, lanes] = (h * cdf).astype(BF)
            gp[q, j, :, lanes] = (cdf + h * (jnp.exp(-0.5 * h * h) * norm_pdf)).astype(BF)
            return carry

        lax.fori_loop(0, 8, body, 0)

    def units_out(j, src, buf):
        def body(dn, cols):
            acc = dot(src[0, j], rows_at(buf, 0, dn, 0, 1024), 1, 1)
            acc = acc + dot(src[1, j], rows_at(buf, 1, dn, 0, 1024), 1, 1)
            sx[j, :, cols] = acc.astype(BF)

        over_columns(body)

    run("ye2")
    c_event("e")
    hidden_units(0)
    run("zs2", "ys-1", "ys0")
    hidden_units(1)
    run("ys1", "ys2")
    c_event("s")
    units_out(0, gg, ws)
    exchange(2, 0)
    units_out(1, gg, ws)
    exchange(2, 1)
    l_c.wait()
    xs[2].wait_recv()

    def last_norm(j):
        arrived(2, j)
        gain, shift, bias = gains[2], biases[8], biases[5]

        def body(i, carry):
            sa, sb, sc = carry
            rws = pl.ds(pl.multiple_of(i * TILE, TILE), TILE)
            v = res[j, rws, :] + sx[j, rws, :].astype(F32) + rx[0, j, rws, :].astype(F32) + bias
            cen = v - jnp.mean(v, axis=1, keepdims=True)
            r = lax.rsqrt(jnp.mean(cen * cen, axis=1, keepdims=True) + EPS)
            n = cen * r
            xt[rws, :] = (n * gain + shift).astype(BF)
            dz = ct[j, rws, :].astype(F32)
            dt = back_tile(dz, n, r, gain)
            res[j, rws, :] = dt
            ct[j, rws, :] = dt.astype(BF)
            return sa + fold(dz * n), sb + fold(dz), sc + fold(dt)

        zero = jnp.zeros((8, 1024), F32)
        sa, sb, sc = lax.fori_loop(0, rows // TILE, body, (zero, zero, zero))
        add_small(2, sa)
        add_small(11, sb)
        add_small(8, sc)

        @pl.when(x == j)
        def _():
            local(xt, block_out).wait()

    def units_back(j):
        def body(step, carry):
            q, i = step // 4, step % 4
            lanes = pl.ds(pl.multiple_of(i * 256, 256), 256)
            g = dot(ct[j], ws[q, :, :, :, lanes].reshape(1024, 256), 1, 0)
            g = (g * gp[q, j, :, lanes].astype(F32)).astype(BF)
            gp[q, j, :, lanes] = g
            sm[pl.ds(13 + 2 * x + q, 1), lanes] += jnp.sum(g.astype(F32), axis=0, keepdims=True)
            return carry

        lax.fori_loop(0, 8, body, 0)
        units_out(j, gp, we)
        exchange(3, j)

    last_norm(0)
    units_back(0)
    last_norm(1)
    units_back(1)

    def grad_into(dst, pieces, first=0):
        def body(i, carry):
            lanes = pl.ds(pl.multiple_of(i * 256, 256), 256)
            lo = first
            for left, right in pieces:
                g = dot(left[:, :, lanes].reshape(512, 256), right, 0, 0)
                w = g.shape[1]
                dst[pl.ds(i * nq, nq), :, :, lo : lo + w] = g.astype(BF).reshape(nq, 2, sh, w)
                lo += w
            return carry

        lax.fori_loop(0, 4, body, 0)

    own_of = {0: own.at[0], 1: own.at[1], 2: we.at[0], 3: we.at[1]}
    send_of = {0: ws.at[0], 1: ws.at[1], 2: ws.at[0], 3: ws.at[1]}
    units = [(0, 0, 1024), (1, 0, 1024), (2, 0, 256), (2, 256, 1024)] + [(3, 256 * p, 256 * p + 256) for p in range(4)]
    z_to = {k: lax.rem(z + k, nz) for k in peers_z}
    gsend, gy, gz_ = [], [], []
    for g, lo, hi in units:
        gsend.append(plan(send_of[g].at[:, :, :, lo:hi], cland.at[g, :, :, :, lo:hi], c_dev))
        gy.append(plan(own_of[g].at[:, ny, :, lo:hi], yland.at[g, :, :, lo:hi], y_dev))
        gz_.append([plan(own_of[g].at[z_to[k], y, :, lo:hi], zland.at[g, k, :, lo:hi], z_dev(k)) for k in peers_z])

    def unit_pair(ref, q):
        return ref[q].reshape(512, 1024)

    for g in ("e", "s"):
        for kind in (zc, yc, cz, cy):
            for cp in kind[g].values():
                sent(cp)
    grad_into(send_of[0], [(x2r, unit_pair(gp, nc))])
    launch(gsend[0])
    grad_into(own_of[0], [(x2r, unit_pair(gp, c))])
    grad_into(send_of[1], [(ct, unit_pair(gg, nc))])
    launch(gsend[1])
    grad_into(own_of[1], [(ct, unit_pair(gg, c))])
    l_en2a = local(enc, x2r.at[x])
    l_en2b = local(eland.at[nx], x2r.at[nx])


    def grad_core(u):
        g, lo, hi = units[u]
        gsend[u].wait_recv()
        local(cland.at[g, :, :, :, lo:hi], tmp.at[:, :, :, lo:hi]).wait()
        o = own_of[g]

        def body(i, carry):
            blk = pl.ds(i * nq, nq)
            o[blk, :, :, lo:hi] = (o[blk, :, :, lo:hi].astype(F32) + tmp[blk, :, :, lo:hi].astype(F32)).astype(BF)
            return carry

        lax.fori_loop(0, 4, body, 0)
        launch(gy[u])

    def grad_y(u):
        g, lo, hi = units[u]
        gy[u].wait_recv()
        local(yland.at[g, :, :, lo:hi], tmp.at[:, 0, :, lo:hi]).wait()
        o = own_of[g]

        def body(i, carry):
            blk = pl.ds(i * nq, nq)
            o[blk, y, :, lo:hi] = (o[blk, y, :, lo:hi].astype(F32) + tmp[blk, 0, :, lo:hi].astype(F32)).astype(BF)
            return carry

        lax.fori_loop(0, 4, body, 0)
        for cp in gz_[u]:
            launch(cp)

    out_copies = {}

    def grad_z(u, out):
        g, lo, hi = units[u]
        cps = []
        for k in peers_z:
            gz_[u][k - 1].wait_recv()
            cps.append(local(zland.at[g, k, :, lo:hi], tmp.at[k, 0, :, lo:hi]))
        for cp in cps:
            cp.wait()
        acc = own_of[g][z, y, :, lo:hi].astype(F32)
        for k in peers_z:
            acc = acc + tmp[k, 0, :, lo:hi].astype(F32)
        spot = outf.at[g % 2, :, lo:hi]
        for key in [key for key in out_copies if key[0] == g - 2]:
            out_copies.pop(key).wait()
        spot[...] = acc
        if g == 0:
            local(spot, out.at[:, lo:hi]).wait()
        else:
            out_copies[g, lo] = local(spot, out.at[:, lo:hi])

    def sum_rows(row, src, col):
        sm[row : row + 1, pl.ds(pl.multiple_of(col, 256), 256)] += jnp.sum(src.astype(F32), axis=0, keepdims=True)

    def heads_back(j, buf, lo, q_ref, k_ref, v_ref, o_ref, l_ref, causal, hooks):
        def body(q, carry):
            do[:, pl.ds(pl.multiple_of(q * 256, 256), 256)] = dot(ct[j], w_all(buf, q, lo, lo + 256), 1, 0).astype(BF)
            return carry

        lax.fori_loop(0, 2, body, 0)
        attend_back(j, q_ref, k_ref, v_ref, o_ref, l_ref, causal, hooks)

    def swap_kv(slot):
        for j in range(2):
            ksend[0, j] = dk[2 * j + nc].astype(BF)
            ksend[1, j] = dv[2 * j + nc].astype(BF)
        return send(ksend, krecv.at[slot], c_dev)

    def join_kv(slot):
        for j in range(2):
            krecv[slot, 0, j] = (dk[2 * j + c] + krecv[slot, 0, j].astype(F32)).astype(BF)
            krecv[slot, 1, j] = (dv[2 * j + c] + krecv[slot, 1, j].astype(F32)).astype(BF)

    def head_cols(ref, q):
        return ref[:, :, pl.ds(pl.multiple_of(q * 256, 256), 256)].reshape(512, 256)

    def cross_back(j, hooks):
        arrived(3, j)
        norm_back(j, 3, gains[1], n2, r2, 1, 10, 7)
        if j == 1:
            sent(gsend[0])
            grad_into(send_of[2], [(ct, head_cols(a2, nc))])
            launch(gsend[2])
            grad_into(own_of[2], [(ct, head_cols(a2, c))])
        heads_back(j, wc, 256, q2, k2, v2, a2, lse2, False, hooks)
        project_out(j, dq, wc, 0)
        exchange(4, j)

    part = functools.partial
    grad_core(0)
    cross_back(0, ({}, {2: part(grad_core, 1)}))
    cross_back(1, ({6: part(grad_y, 0)}, {4: part(grad_core, 2)}))
    swap2 = swap_kv(0)
    for j in range(2):
        for q in range(2):
            sum_rows(5, dq[j, :, q * 256 : q * 256 + 256], x * 512 + q * 256)
    swap2.wait_recv()
    join_kv(0)
    for j in range(2):
        for q in range(2):
            sum_rows(6, krecv[0, 1, j, :, q * 256 : q * 256 + 256], x * 512 + q * 256)
    l_en2a.wait()
    l_en2b.wait()

    def cross_pieces(q):
        return [
            (x1r, head_cols(dq, q)),
            (x2r, head_cols(krecv.at[0, 0], q)),
            (x2r, head_cols(krecv.at[0, 1], q)),
        ]

    grad_into(send_of[2], cross_pieces(nc), 256)
    launch(gsend[3])
    grad_into(own_of[2], cross_pieces(c), 256)
    l_x2a = local(hid, x1r.at[x])
    l_x2b = local(xland.at[nx], x1r.at[nx])

    def input_part(j, terms, dn):
        acc = None
        for ref, buf, lo in terms:
            for q in range(2):
                part = dot(ref[j, :, q * 256 : q * 256 + 256], rows_at(buf, q, dn, lo, lo + 256), 1, 1)
                acc = part if acc is None else acc + part
        return acc

    enc_terms = [(krecv.at[0, 0], wb, 256), (krecv.at[0, 1], wb, 512)]
    def part_of_enc_terms_xt(dn, cols):
        xt[:, cols] = input_part(nx, enc_terms, dn).astype(BF)

    over_columns(part_of_enc_terms_xt)
    def part_of_enc_terms_den(dn, cols):
        den[:, cols] = input_part(x, enc_terms, dn)

    over_columns(part_of_enc_terms_den)
    enc_x = send(xt, rxd.at[0], x_dev)

    def self_back(j, hooks):
        arrived(4, j)
        norm_back(j, 4, gains[0], n1, r1, 0, 9, 12)
        if j == 1:
            sent(gsend[1])
            grad_into(send_of[3], [(ct, head_cols(ao, nc))])
            launch(gsend[4])
            grad_into(own_of[3], [(ct, head_cols(ao, c))])
        heads_back(j, wb, 0, qs, ks, vs, ao, lse1, True, hooks)

    self_back(0, ({1: part(grad_core, 3), 6: part(grad_y, 1)}, {6: part(grad_y, 2)}))
    sent(enc_x)
    self_back(1, ({5: part(grad_core, 4)}, {2: part(grad_z, 0, ge_out)}))
    sent(swap2)
    swap1 = swap_kv(1)
    l_x2a.wait()
    l_x2b.wait()
    grad_into(send_of[3], [(x1r, head_cols(dq, nc))], 256)
    launch(gsend[5])
    grad_into(own_of[3], [(x1r, head_cols(dq, c))], 256)
    for j in range(2):
        for q in range(2):
            sum_rows(3, dq[j, :, q * 256 : q * 256 + 256], x * 512 + q * 256)
    swap1.wait_recv()
    join_kv(1)
    grad_into(send_of[3], [(x1r, head_cols(krecv.at[1, i], nc)) for i in range(2)], 512)
    launch(gsend[6])
    launch(gsend[7])
    grad_core(5)
    grad_y(3)
    in_terms = [(dq, wa, 0), (krecv.at[1, 0], wa, 256), (krecv.at[1, 1], wa, 512)]
    def part_of_in_terms_xt(dn, cols):
        xt[:, cols] = input_part(nx, in_terms, dn).astype(BF)

    over_columns(part_of_in_terms_xt)
    hid_x = send(xt, rxd.at[1], x_dev)
    grad_into(own_of[3], [(x1r, head_cols(krecv.at[1, i], c)) for i in range(2)], 512)
    grad_core(6)
    grad_core(7)
    for j in range(2):
        for q in range(2):
            sum_rows(4, krecv[1, 1, j, :, q * 256 : q * 256 + 256], x * 512 + q * 256)
    s1 = send(sm, smr.at[0], c_dev)
    grad_y(4)
    def part_of_in_terms_res(dn, cols):
        res[x, :, cols] += input_part(x, in_terms, dn)

    over_columns(part_of_in_terms_res)
    s1.wait_recv()
    sent(s1)
    sm[...] += smr[0]
    s2 = send(sm, smr.at[1], x_dev)
    sent(hid_x)
    enc_x.wait_recv()
    den[...] += rxd[0].astype(F32)
    o1 = local(den, enc_out)
    grad_y(5)
    s2.wait_recv()
    sent(s2)
    sm[...] += smr[1]
    s3 = send(sm, smr.at[2], y_dev)
    grad_z(1, gs_out)
    hid_x.wait_recv()
    res[x] += rxd[1].astype(F32)
    o2 = local(res.at[x], hid_out)
    grad_y(6)
    s3.wait_recv()
    sent(s3)
    sm[...] += smr[2]
    smz[z] = sm[...]
    s4 = [send(sm, smz.at[z], z_dev(k)) for k in range(1, nz)]
    grad_y(7)
    grad_z(2, gc_out)
    grad_z(3, gc_out)
    grad_z(4, ga_out)
    grad_z(5, ga_out)
    for cp in s4:
        cp.wait_recv()
        sent(cp)
    acc = smz[0]
    for k in range(1, nz):
        acc = acc + smz[k]
    for row in range(3):
        gain_out[row] = acc[row : row + 1, :]
    for row in range(9):
        bias_out[row] = acc[row + 3 : row + 4, :]
    selfb_out[...] = acc[12:13, :]
    for row in range(4):
        expb_out[:, row * 1024 : row * 1024 + 1024] = acc[row + 13 : row + 14, :]
    grad_z(6, ga_out)
    grad_z(7, ga_out)
    for cp in [o1, o2] + list(out_copies.values()):
        cp.wait()
    for cp in list(pending):
        sent(cp)


def run_layer(nz, sh, prefix, hid, enc, cot, shards, gains, biases, selfb, expb):
    any_spec = pl.BlockSpec(memory_space=pl.ANY)
    vmem = pl.BlockSpec(memory_space=pltpu.VMEM)
    rows = hid.shape[0]
    shape = jax.ShapeDtypeStruct
    outs = [
        shape((rows, 1024), BF),
        shape((rows, 1024), F32),
        shape((rows, 1024), F32),
        shape((sh, 1024), F32),
        shape((sh, 1024), F32),
        shape((sh, 1024), F32),
        shape((sh, 1024), F32),
        shape((3, 1, 1024), F32),
        shape((9, 1, 1024), F32),
        shape((1, 1024), F32),
        shape((1, 4096), F32),
        shape((2, rows, 1024), BF),
        shape((2, rows, 1024), BF),
        shape((4, nz, 2, sh, 1024), BF),
        shape((4, nz, sh, 1024), BF),
        shape((4, nz, sh, 1024), BF),
    ]

    def weight(n):
        return pltpu.VMEM((2, nz, 2, sh, n), BF)

    def acts(n, kind=BF):
        return pltpu.VMEM((2, rows, n), kind)

    def keys(kind=BF):
        return pltpu.VMEM((4, rows, 512), kind)

    scratch = [
        weight(768),
        weight(768),
        weight(512),
        weight(1024),
        weight(1024),
        acts(1024),
        acts(1024),
        acts(1024),
        acts(512),
        keys(),
        keys(),
        acts(512),
        acts(512),
        keys(),
        keys(),
        acts(512),
        pltpu.VMEM((2, 2, rows, 1024), BF),
        pltpu.VMEM((2, 2, rows, 1024), BF),
        acts(1024),
        acts(1024),
        acts(128, F32),
        acts(128, F32),
        acts(128, F32),
        acts(128, F32),
        acts(1024, F32),
        acts(1024),
        pltpu.VMEM((2, 2, rows, 1024), BF),
        acts(1024),
        acts(512),
        pltpu.VMEM((rows, 512), BF),
        keys(F32),
        keys(F32),
        pltpu.VMEM((2, 2, rows, 512), BF),
        pltpu.VMEM((2, 2, 2, rows, 512), BF),
        pltpu.VMEM((2, 1024, 1024), BF),
        pltpu.VMEM((2, nz, 2, sh, 1024), BF),
        pltpu.VMEM((nz, 2, sh, 1024), BF),
        pltpu.VMEM((rows, 1024), BF),
        pltpu.VMEM((1024, 256), BF),
        pltpu.VMEM((1024, 256), BF),
        pltpu.VMEM((rows, 1024), F32),
        pltpu.VMEM((2, sh, 1024), F32),
        pltpu.VMEM((SMALL_ROWS, 1024), F32),
        pltpu.VMEM((3, SMALL_ROWS, 1024), F32),
        pltpu.VMEM((nz, SMALL_ROWS, 1024), F32),
        pltpu.SemaphoreType.DMA((280 + 64 * nz,)),
    ]
    return pl.pallas_call(
        functools.partial(layer_kernel, nz, sh),
        out_shape=outs,
        in_specs=[pl.BlockSpec(memory_space=pltpu.SMEM)] + [any_spec] * 13 + [vmem] * 4,
        out_specs=[any_spec] * 7 + [vmem] * 4 + [any_spec] * (len(outs) - 11),
        scratch_shapes=scratch,
        compiler_params=pltpu.CompilerParams(
            collective_id=0, has_side_effects=True, vmem_limit_bytes=67043328
        ),
    )(prefix, hid, enc, cot, *shards, gains, biases, selfb, expb)


def per_device(
    hidden,
    encoder,
    prefix,
    query_self,
    key_self,
    value_self,
    output_self,
    cross_query_matrix,
    key_cross,
    value_cross,
    output_cross,
    expand,
    shrink,
    norm_gains,
    biases,
    self_out_bias,
    expand_bias,
    cotangent,
):
    sh = query_self.shape[1]
    nz = 1024 // sh // 2
    shards = (
        query_self[0],
        key_self[0],
        value_self[0],
        output_self[0].T,
        key_cross[0],
        value_cross[0],
        cross_query_matrix[0],
        output_cross[0].T,
        expand[0],
        shrink[0].T,
    )
    outs = run_layer(
        nz,
        sh,
        prefix,
        hidden[0],
        encoder[0],
        cotangent[0],
        shards,
        jnp.swapaxes(norm_gains, 0, 1),
        jnp.swapaxes(biases, 0, 1),
        self_out_bias,
        expand_bias,
    )
    block, grad_hid, grad_enc, ge, gs, gc, ga, gain, bias, selfb, expb = outs[:11]

    def part(g, i):
        return g[:, i * 256 : i * 256 + 256]

    return (
        block[None],
        grad_hid[None],
        grad_enc[None],
        part(ga, 1)[None],
        part(ga, 2)[None],
        part(ga, 3)[None],
        part(ga, 0).T[None],
        part(gc, 1)[None],
        part(gc, 2)[None],
        part(gc, 3)[None],
        part(gc, 0).T[None],
        ge[None],
        gs.T[None],
        jnp.swapaxes(gain, 0, 1),
        jnp.swapaxes(bias, 0, 1),
        selfb,
        expb,
    )


def solution(mesh):
    in_specs = (
        P("dp", "tensor", None),
        P("dp", "tensor", None),
        P("dp"),
        P(None, "dp", "tensor"),
        P(None, "dp", "tensor"),
        P(None, "dp", "tensor"),
        P(None, "tensor", "dp"),
        P(None, "dp", "tensor"),
        P(None, "dp", "tensor"),
        P(None, "dp", "tensor"),
        P(None, "tensor", "dp"),
        P(None, "dp", "tensor"),
        P(None, "tensor", "dp"),
        P(),
        P(),
        P(),
        P(),
        P("dp", "tensor", None),
    )
    out_specs = (
        P("dp", "tensor", None),
        P("dp", "tensor", None),
        P("dp", "tensor", None),
        P(None, "dp", "tensor"),
        P(None, "dp", "tensor"),
        P(None, "dp", "tensor"),
        P(None, "tensor", "dp"),
        P(None, "dp", "tensor"),
        P(None, "dp", "tensor"),
        P(None, "dp", "tensor"),
        P(None, "tensor", "dp"),
        P(None, "dp", "tensor"),
        P(None, "tensor", "dp"),
        P(),
        P(),
        P(),
        P(),
    )
    return jax.shard_map(
        per_device, mesh=mesh, in_specs=in_specs, out_specs=out_specs, check_vma=False
    )
```

profile of v0, /device:TPU:0, one launch (start us, length us, event | category | flops | bytes accessed | tf_op | source)
XLA Modules:
  0.0 325.3 jit_solution(4376087227676419907)
XLA Ops:
  1.3 1.6 copy.35
  2.9 1.6 copy.36
  4.4 1.8 copy.37
  6.2 306.0 %shard_map.305 = (bf16[256,1024]{1,0:T(8,128)(2,1)}, f32[256,1024]{1,0:T(8,128)}, f32[256,1024]{1,0:T(8,128)}, f32[128,1024]{1,0:T(8,128)}, f32[128,1024]{1,0:T(...) custom-call(s32[1]{0:T(128)S(6)} %copy.49.refs_0_, ...), custom_call_target="tpu_custom_call" | custom-call | tf_op jit(solution)/shard_map/pallas_call | solution.py:964
  312.3 0.0 copy-start.1
  312.3 0.0 copy-start
  312.3 2.2 copy.40
  314.5 0.0 copy-start.2
  314.5 0.0 copy-start.5
  314.5 0.0 copy-start.3
  314.5 0.0 copy-start.6
  314.5 0.0 copy-start.4
  314.5 2.2 slice_bitcast_fusion
  316.7 0.8 copy.39
  317.5 0.8 copy.38
  318.2 1.9 copy.50
  320.1 0.0 copy-done.1
  320.1 1.0 copy.51
  321.1 0.0 copy-done
  321.1 1.0 copy.52
  322.0 0.0 copy-done.2
  322.0 0.8 copy.53
  322.8 0.0 copy-done.5
  322.8 0.6 copy.54
  323.4 0.0 copy-done.3
  323.4 0.6 copy.55
  324.1 0.0 copy-done.6
  324.1 0.6 copy.56
  324.6 0.0 copy-done.4
  324.7 0.6 copy.57
Async XLA Ops:
  312.3 7.8 %copy-start.1 = (f32[256,1024]{1,0:T(8,128)S(1)}, f32[256,1024]{1,0:T(8,128)}, u32[]{:S(2)}) copy-start(f32[256,1024]{1,0:T(8,128)} %get-tuple-element.29) | copy-start | bytes 3145732
  312.3 8.8 %copy-start = (f32[256,1024]{1,0:T(8,128)S(1)}, f32[256,1024]{1,0:T(8,128)}, u32[]{:S(2)}) copy-start(f32[256,1024]{1,0:T(8,128)} %get-tuple-element.30) | copy-start | bytes 3145732
  314.5 7.6 %copy-start.2 = (f32[128,1024]{1,0:T(8,128)S(1)}, f32[128,1024]{1,0:T(8,128)}, u32[]{:S(2)}) copy-start(f32[128,1024]{1,0:T(8,128)} %get-tuple-element.33) | copy-start | bytes 1572868
  314.5 8.4 %copy-start.5 = (f32[3,1,1024]{2,1,0:T(1,128)S(1)}, f32[3,1,1024]{2,1,0:T(1,128)}, u32[]{:S(2)}) copy-start(f32[3,1,1024]{2,1,0:T(1,128)} %get-tuple-element.35) | copy-start | bytes 36868
  314.5 9.0 %copy-start.3 = (f32[9,1,1024]{2,1,0:T(1,128)S(1)}, f32[9,1,1024]{2,1,0:T(1,128)}, u32[]{:S(2)}) copy-start(f32[9,1,1024]{2,1,0:T(1,128)} %get-tuple-element.36) | copy-start | bytes 110596
  314.5 9.6 %copy-start.6 = (f32[1,1024]{1,0:T(1,128)S(1)}, f32[1,1024]{1,0:T(1,128)}, u32[]{:S(2)}) copy-start(f32[1,1024]{1,0:T(1,128)} %get-tuple-element.100) | copy-start | bytes 12292
  314.5 10.2 %copy-start.4 = (f32[1,4096]{1,0:T(1,128)S(1)}, f32[1,4096]{1,0:T(1,128)}, u32[]{:S(2)}) copy-start(f32[1,4096]{1,0:T(1,128)} %get-tuple-element.101) | copy-start | bytes 49156
where the time goes:
time: 329 us; the launch traced here: 325 us
  Pallas kernels  306 us (93%)
  local copies, waits for them, and re-layouts  17.9 us (5%)
    pallas_call x1, Pallas kernels, run_layer(): pl.pallas_call(functools.partial(layer_kernel, nz, sh), out_shape=outs, i...  306 us
    unnamed x28, local copies, waits for them, and re-layouts  15.7 us

commit v1 on v0

--- a/solution.py
+++ b/solution.py
@@ -477,15 +477,15 @@
 
     for cp in kv1:
         cp.wait_recv()
-    attend(0, qs, ks, vs, ao, lse1, True, {5: ("zb2",), 14: ("zc0", "os",)})
-    run("yb-1", "yb0", "yb1", "zc1", "yb2")
+    attend(0, qs, ks, vs, ao, lse1, True, {8: ("zb2",)})
+    run("yb-1", "yb0", "zc0", "os", "yb1", "yb2")
     c_event("b")
     project_out(0, ao, wb, 0)
     exchange(0, 0)
-    attend(1, qs, ks, vs, ao, lse1, True, {4: ("zc2",), 13: ("yc-1", "yc0",)})
+    attend(1, qs, ks, vs, ao, lse1, True, {2: ("zc1",), 12: ("zc2",)})
     project_out(1, ao, wb, 0)
     exchange(0, 1)
-    run("ze0", "yc1", "yc2")
+    run("yc-1", "yc0")
     l_e.wait()
     l_en.wait()
     def encoder_part(i, carry):
@@ -497,6 +497,7 @@
         return carry
 
     lax.fori_loop(0, 4, encoder_part, 0)
+    run("ze0", "yc1", "yc2")
     kv2 = [send(b.at[2 * j + c], b.at[2 * j + c], c_dev) for j in range(2) for b in (k2, v2)]
     c_event("c")
     for cp in kv2:
@@ -516,8 +517,8 @@
         project_out(j, a2, wc, 256)
         exchange(1, j)
 
-    cross(0, {1: ("ze1",), 12: ("ze2",)})
-    cross(1, {1: ("zs0",), 6: ("ye-1", "ye0", "ye1",), 12: ("zs1",)})
+    cross(0, {4: ("ze1",), 14: ("ze2",)})
+    cross(1, {4: ("ye-1", "ye0", "zs0",), 14: ("zs1", "ye1")})
 
     root_half = 0.7071067811865476
     norm_pdf = 0.3989422804014327
@@ -738,7 +739,7 @@
     part = functools.partial
     grad_core(0)
     cross_back(0, ({}, {2: part(grad_core, 1)}))
-    cross_back(1, ({6: part(grad_y, 0)}, {4: part(grad_core, 2)}))
+    cross_back(1, ({}, {2: part(grad_y, 0), 6: part(grad_core, 2)}))
     swap2 = swap_kv(0)
     for j in range(2):
         for q in range(2):
@@ -793,9 +794,9 @@
             grad_into(own_of[3], [(ct, head_cols(ao, c))])
         heads_back(j, wb, 0, qs, ks, vs, ao, lse1, True, hooks)
 
-    self_back(0, ({1: part(grad_core, 3), 6: part(grad_y, 1)}, {6: part(grad_y, 2)}))
+    self_back(0, ({2: part(grad_core, 3)}, {2: part(grad_y, 1)}))
     sent(enc_x)
-    self_back(1, ({5: part(grad_core, 4)}, {2: part(grad_z, 0, ge_out)}))
+    self_back(1, ({2: part(grad_y, 2), 6: part(grad_core, 4)}, {4: part(grad_z, 0, ge_out)}))
     sent(swap2)
     swap1 = swap_kv(1)
     l_x2a.wait()

time: 329 us -> 323 us (0.982)
  Pallas kernels: 306 us -> 302 us
    pallas_call x1, Pallas kernels: 306 us -> 302 us  [run_layer(): pl.pallas_call(functools.partial(layer_kernel, nz, sh), out_shape=outs, i...]
where the time goes in v1:
time: 323 us; the launch traced here: 321 us
  Pallas kernels  302 us (93%)
  local copies, waits for them, and re-layouts  17.9 us (6%)
    pallas_call x1, Pallas kernels, run_layer(): pl.pallas_call(functools.partial(layer_kernel, nz, sh), out_shape=outs, i...  302 us
    unnamed x28, local copies, waits for them, and re-layouts  15.7 us

profile of v1, /device:TPU:0, one launch (start us, length us, event | category | flops | bytes accessed | tf_op | source)
XLA Modules:
  0.0 321.2 jit_solution(13189587333211236208)
XLA Ops:
  1.3 1.6 copy.35
  2.9 1.6 copy.36
  4.4 1.8 copy.37
  6.2 301.9 %shard_map.305 = (bf16[256,1024]{1,0:T(8,128)(2,1)}, f32[256,1024]{1,0:T(8,128)}, f32[256,1024]{1,0:T(8,128)}, f32[128,1024]{1,0:T(8,128)}, f32[128,1024]{1,0:T(...) custom-call(s32[1]{0:T(128)S(6)} %copy.49.refs_0_, ...), custom_call_target="tpu_custom_call" | custom-call | tf_op jit(solution)/shard_map/pallas_call | solution.py:965
  308.2 0.0 copy-start.1
  308.2 0.0 copy-start
  308.2 2.2 copy.40
  310.4 0.0 copy-start.2
  310.4 0.0 copy-start.5
  310.4 0.0 copy-start.3
  310.4 0.0 copy-start.6
  310.4 0.0 copy-start.4
  310.4 2.2 slice_bitcast_fusion
  312.6 0.8 copy.39
  313.4 0.8 copy.38
  314.1 1.9 copy.50
  316.0 0.0 copy-done.1
  316.0 1.0 copy.51
  317.0 0.0 copy-done
  317.0 1.0 copy.52
  317.9 0.0 copy-done.2
  317.9 0.8 copy.53
  318.7 0.0 copy-done.5
  318.7 0.6 copy.54
  319.3 0.0 copy-done.3
  319.3 0.6 copy.55
  320.0 0.0 copy-done.6
  320.0 0.6 copy.56
  320.6 0.0 copy-done.4
  320.6 0.6 copy.57
Async XLA Ops:
  308.2 7.8 %copy-start.1 = (f32[256,1024]{1,0:T(8,128)S(1)}, f32[256,1024]{1,0:T(8,128)}, u32[]{:S(2)}) copy-start(f32[256,1024]{1,0:T(8,128)} %get-tuple-element.29) | copy-start | bytes 3145732
  308.2 8.8 %copy-start = (f32[256,1024]{1,0:T(8,128)S(1)}, f32[256,1024]{1,0:T(8,128)}, u32[]{:S(2)}) copy-start(f32[256,1024]{1,0:T(8,128)} %get-tuple-element.30) | copy-start | bytes 3145732
  310.4 7.6 %copy-start.2 = (f32[128,1024]{1,0:T(8,128)S(1)}, f32[128,1024]{1,0:T(8,128)}, u32[]{:S(2)}) copy-start(f32[128,1024]{1,0:T(8,128)} %get-tuple-element.33) | copy-start | bytes 1572868
  310.4 8.4 %copy-start.5 = (f32[3,1,1024]{2,1,0:T(1,128)S(1)}, f32[3,1,1024]{2,1,0:T(1,128)}, u32[]{:S(2)}) copy-start(f32[3,1,1024]{2,1,0:T(1,128)} %get-tuple-element.35) | copy-start | bytes 36868
  310.4 9.0 %copy-start.3 = (f32[9,1,1024]{2,1,0:T(1,128)S(1)}, f32[9,1,1024]{2,1,0:T(1,128)}, u32[]{:S(2)}) copy-start(f32[9,1,1024]{2,1,0:T(1,128)} %get-tuple-element.36) | copy-start | bytes 110596
  310.4 9.6 %copy-start.6 = (f32[1,1024]{1,0:T(1,128)S(1)}, f32[1,1024]{1,0:T(1,128)}, u32[]{:S(2)}) copy-start(f32[1,1024]{1,0:T(1,128)} %get-tuple-element.100) | copy-start | bytes 12292
  310.4 10.2 %copy-start.4 = (f32[1,4096]{1,0:T(1,128)S(1)}, f32[1,4096]{1,0:T(1,128)}, u32[]{:S(2)}) copy-start(f32[1,4096]{1,0:T(1,128)} %get-tuple-element.101) | copy-start | bytes 49156
